TPU v7x, 32 devices: a whole 2x2x4 slice. The times are simulated.
32 devices in a mesh: gx: 8 (over z, y), gy: 4 (over x, core).
Axes of the slice: x: 2, y: 2, z: 4, core: 2. Of those that a mesh axis runs over, the one named last changes fastest.
Arguments:
- electric: float32 [3, 128, 512, 128], P(None, 'gx', 'gy'), may hold values from -6 to 6
- magnetic: float32 [3, 128, 512, 128], P(None, 'gx', 'gy'), may hold values from -6 to 6
- retention: float32 [128, 512, 128], P('gx', 'gy'), may hold values from 0.5 to 1
- coupling: float32 [128, 512, 128], P('gx', 'gy'), may hold values from 0.1 to 0.5
- spectrum_real: float32 [4, 4, 128, 512], P(None, None, 'gx', 'gy'), may hold values from -6 to 6
- spectrum_imag: float32 [4, 4, 128, 512], P(None, None, 'gx', 'gy'), may hold values from -6 to 6
- phases: float32 [4], replicated, may hold values from -3.140625 to 3.140625
Outputs:
- next_electric: float32 [3, 128, 512, 128], P(None, 'gx', 'gy')
- next_magnetic: float32 [3, 128, 512, 128], P(None, 'gx', 'gy')
- next_real: float32 [4, 4, 128, 512], P(None, None, 'gx', 'gy')
- next_imag: float32 [4, 4, 128, 512], P(None, None, 'gx', 'gy')
- far_field: float32 [2, 4, 4, 256, 256], P(None, None, None, 'gx', 'gy')
All inputs are finite; a program needn't handle non-finite values.
Results may differ from a plain program's by a relative error of at most 0.000071.
Values sent between devices are 32-bit elements; how exact they have to be, the bound alone decides.
No kernel may reach another device: no remote copies, remote signals or barrier semaphores. Data moves between devices by JAX's collectives and lax.ppermute only.
A program may use at most 128 MiB of HBM per device.

v0:
```python
import math
import jax
import jax.numpy as jnp
from jax import lax
from jax.sharding import PartitionSpec as P

WAVES = 256
TOP_PLANE = 111
curl_step = 0.5


def passed_along(value, axis, by):
    devices = lax.axis_size(axis)
    pairs = [(i, i + by) for i in range(devices) if 0 <= i + by < devices]
    return lax.ppermute(value, axis, pairs)


def forward_diff(values, along):
    padded = jnp.pad(values, [(0, 1) if which == along else (0, 0) for which in range(values.ndim)])
    return lax.slice_in_dim(padded, 1, values.shape[along] + 1, axis=along) - values


def backward_diff(values, along):
    padded = jnp.pad(values, [(1, 0) if which == along else (0, 0) for which in range(values.ndim)])
    return values - lax.slice_in_dim(padded, 0, values.shape[along], axis=along)


def ahead_diff(values, border, along):
    upper = lax.slice_in_dim(values, 1, values.shape[along], axis=along)
    return jnp.concatenate([upper, border], axis=along) - values


def behind_diff(values, border, along):
    lower = lax.slice_in_dim(values, 0, values.shape[along] - 1, axis=along)
    return values - jnp.concatenate([border, lower], axis=along)


def tables(number, extent, offset):
    wave = 2 * jnp.arange(number, dtype=jnp.int32) + 1 - number
    places = offset + jnp.arange(extent, dtype=jnp.int32)
    folded = wave[:, None] * places[None, :] % (4 * number)
    angles = folded.astype(jnp.float32) * (math.pi / (2 * number))
    return (jnp.cos(angles), jnp.sin(angles))


def first_section(real_part, imag_part, cos_y, sin_y):
    highest = lax.Precision.HIGHEST
    part_real = jnp.einsum("cfxy,ky->cfxk", real_part, cos_y, precision=highest) + jnp.einsum(
        "cfxy,ky->cfxk", imag_part, sin_y, precision=highest
    )
    part_imag = jnp.einsum("cfxy,ky->cfxk", imag_part, cos_y, precision=highest) - jnp.einsum(
        "cfxy,ky->cfxk", real_part, sin_y, precision=highest
    )
    return (part_real, part_imag)


def second_section(part_real, part_imag, cos_x, sin_x):
    highest = lax.Precision.HIGHEST
    far_real = jnp.einsum("jx,cfxk->cfjk", cos_x, part_real, precision=highest) + jnp.einsum(
        "jx,cfxk->cfjk", sin_x, part_imag, precision=highest
    )
    far_imag = jnp.einsum("jx,cfxk->cfjk", cos_x, part_imag, precision=highest) - jnp.einsum(
        "jx,cfxk->cfjk", sin_x, part_real, precision=highest
    )
    return jnp.stack([far_real, far_imag])


def per_device(electric, magnetic, retention, coupling, spectrum_real, spectrum_imag, phases):
    elec_x, elec_y, elec_z = (electric[0], electric[1], electric[2])
    rows_elec = passed_along(electric[1:3, 0:1], "gx", -1)
    cols_elec = passed_along(electric[0:3:2, :, 0:1], "gy", -1)
    mag_x = magnetic[0] - curl_step * (
        ahead_diff(elec_z, cols_elec[1], 1) - forward_diff(elec_y, 2)
    )
    mag_y = magnetic[1] - curl_step * (
        forward_diff(elec_x, 2) - ahead_diff(elec_z, rows_elec[1], 0)
    )
    mag_z = magnetic[2] - curl_step * (
        ahead_diff(elec_y, rows_elec[0], 0) - ahead_diff(elec_x, cols_elec[0], 1)
    )
    next_magnetic = jnp.stack([mag_x, mag_y, mag_z])
    rows_magn = passed_along(next_magnetic[1:3, -1:], "gx", 1)
    cols_magn = passed_along(next_magnetic[0:3:2, :, -1:], "gy", 1)
    new_x = retention * elec_x + coupling * (
        behind_diff(mag_z, cols_magn[1], 1) - backward_diff(mag_y, 2)
    )
    new_y = retention * elec_y + coupling * (
        backward_diff(mag_x, 2) - behind_diff(mag_z, rows_magn[1], 0)
    )
    new_z = retention * elec_z + coupling * (
        behind_diff(mag_y, rows_magn[0], 0) - behind_diff(mag_x, cols_magn[0], 1)
    )
    next_electric = jnp.stack([new_x, new_y, new_z])
    tangent = jnp.stack(
        [
            new_x[:, :, TOP_PLANE],
            new_y[:, :, TOP_PLANE],
            mag_x[:, :, TOP_PLANE],
            mag_y[:, :, TOP_PLANE],
        ]
    )
    next_real = spectrum_real + tangent[:, None] * jnp.cos(phases)[None, :, None, None]
    next_imag = spectrum_imag - tangent[:, None] * jnp.sin(phases)[None, :, None, None]
    local_rows = electric.shape[1]
    local_cols = electric.shape[2]
    scale = 1.0 / math.sqrt(local_rows * lax.axis_size("gx") * local_cols * lax.axis_size("gy"))
    cos_y, sin_y = tables(WAVES, local_cols, lax.axis_index("gy") * local_cols)
    part_real, part_imag = first_section(next_real, next_imag, cos_y, sin_y)
    cos_full, sin_full = tables(WAVES, local_rows * lax.axis_size("gx"), 0)
    reduced = lax.psum_scatter(
        jnp.stack([part_real, part_imag]), "gy", scatter_dimension=4, tiled=True
    )
    columns = lax.all_to_all(reduced, "gx", split_axis=4, concat_axis=3, tiled=True)
    finished = second_section(columns[0], columns[1], cos_full, sin_full)
    whole = lax.all_to_all(finished, "gx", split_axis=3, concat_axis=4, tiled=True)
    far_field = whole * scale
    return (next_electric, next_magnetic, next_real, next_imag, far_field)


def solution(mesh):
    placed = (
        P(None, "gx", "gy", None),
        P(None, "gx", "gy", None),
        P("gx", "gy", None),
        P("gx", "gy", None),
        P(None, None, "gx", "gy"),
        P(None, None, "gx", "gy"),
        P(),
    )
    return jax.shard_map(
        per_device,
        mesh=mesh,
        in_specs=placed,
        out_specs=(
            P(None, "gx", "gy", None),
            P(None, "gx", "gy", None),
            P(None, None, "gx", "gy"),
            P(None, None, "gx", "gy"),
            P(None, None, None, "gx", "gy"),
        ),
        check_vma=False,
    )
```

profile of v0, /device:TPU:0, one launch (start us, length us, event | category | flops | bytes accessed | tf_op | source)
XLA Modules:
  0.0 151.3 jit_solution(2751149047137637543)
XLA Ops:
  7.2 0.9 slice.127
  8.1 1.3 collective-permute-start.1
  9.4 0.9 slice.123
  10.4 1.3 collective-permute-start
  11.7 2.3 %slice_bitcast_fusion.2 = f32[16,128,128]{2,1,0:T(8,128)} fusion(f32[3,16,128,128]{3,2,1,0:T(8,128)} %param.7), kind=kLoop, calls=%fused_computation.58 | loop fusion | bytes 2097152 | tf_op jit(solution)/shard_map/squeeze | solution.py:69
  14.0 3.4 %slice_bitcast_fusion.10 = (f32[15,128,128]{2,1,0:T(8,128)}, f32[1,15,128,128]{3,2,1,0:T(8,128)}, f32[15,128,128]{2,1,0:T(8,128)}) fusion(f32[3,16,128,128]{3,2,1,0:T(8,128)} %param.7), kind=kLoop, calls=%fused_computation.139 | loop fusion | bytes 4915200 | tf_op jit(solution)/shard_map/slice | solution.py:29
  17.5 2.8 %fusion.96 = (f32[16,127,128]{2,1,0:T(8,128)}, f32[1,16,127,128]{3,2,1,0:T(8,128)}) fusion(f32[16,128,128]{2,1,0:T(8,128)} %slice_bitcast_fusion.2), kind=kLoop, calls=%fused_computation.142 | loop fusion | bytes 3121152 | tf_op jit(solution)/shard_map/slice | solution.py:29
  20.4 2.5 %slice_bitcast_fusion = (f32[16,128,128]{2,1,0:T(8,128)S(1)}, f32[1,16,128,128]{3,2,1,0:T(8,128)S(1)}, f32[16,128,128]{2,1,0:T(8,128)S(1)}) fusion(f32[3,16,128,128]{3,2,1,0:T(8,128)S(1)} %copy-done, f32[1,16,1,128]{3,2,1,0:T(1,128)S(1)} %bitcast.155, f32[1,16,127,128]{3,2,1,0:T(8,128)} %get-tuple-element.55, f32[1,1,128,128]{3,2,1,0:T(8,128)S(1)} %get-tuple-element.60, ...), kind=kLoop, calls=%fused_computation.56 | loop fusion | flops 1835008 | bytes 9437184 | tf_op jit(solution)/shard_map/squeeze | solution.py:69
  23.0 0.4 copy-done.6
  23.5 0.3 copy-done.7
  23.8 0.3 copy-done.9
  24.1 0.3 copy-done.10
  24.3 1.8 %fusion.22 = (f32[16,128,128]{2,1,0:T(8,128)S(1)}, f32[16,128,128]{2,1,0:T(8,128)S(1)}, f32[16,128,128]{2,1,0:T(8,128)S(1)}) fusion(f32[1,128,128]{2,1,0:T(8,128)S(1)} %get-tuple-element.58, f32[15,128,128]{2,1,0:T(8,128)S(1)} %copy-done.9, f32[16,1,128]{2,1,0:T(1,128)S(1)} %bitcast.156, f32[16,127,128]{2,1,0:T(8,128)S(1)} %copy-done.7, ...), kind=kLoop, calls=%fused_computation.38 | loop fusion | flops 4980736 | bytes 15728640 | tf_op jit(solution)/shard_map/sub | solution.py:78
  26.1 1.2 slice_reduce_fusion
  27.6 3.3 %collective-permute-start.2 = (f32[2,16,1,128]{3,2,1,0:T(1,128)S(1)}, f32[2,16,1,128]{3,2,1,0:T(1,128)S(1)}, u32[]{:S(2)}, u32[]{:S(2)}) collective-permute-start(f32[2,16,1,128]{3,2,1,0:T(1,128)S(1)} %slice.139), channel_id=1, source_target_pairs={{0,1},{1,2},{2,3},{4,5},{5,6},{6,7},{8,9},{9,10},{10,11},{12,13},{... | collective-permute-start | bytes 49160 | tf_op jit(solution)/shard_map/ppermute | solution.py:15
  31.0 5.7 %collective-permute-start.3 = (f32[2,1,128,128]{3,2,1,0:T(8,128)S(1)}, f32[2,1,128,128]{3,2,1,0:T(8,128)S(1)}, u32[]{:S(2)}, u32[]{:S(2)}) collective-permute-start(f32[2,1,128,128]{3,2,1,0:T(8,128)S(1)} %pad_maximum_fusion.4), channel_id=1, source_target_pairs={{0,4},{4,8},{8,12},{12,16},{16,20},{20,24},{24,28},{1,5},{5,9},{9,... | collective-permute-start | bytes 393224 | tf_op jit(solution)/shard_map/ppermute | solution.py:15
  36.8 2.9 %collective-permute-done.3 = f32[2,1,128,128]{3,2,1,0:T(8,128)S(1)} collective-permute-done((f32[2,1,128,128]{3,2,1,0:T(8,128)S(1)}, f32[2,1,128,128]{3,2,1,0:T(8,128)S(1)}, u32[]{:S(2)}, u32[]{:S(2)}) %collective-permute-start.3) | collective-permute-done | bytes 131104 | tf_op jit(solution)/shard_map/ppermute | solution.py:15
  39.8 2.6 %fusion.15 = (f32[16,128,128]{2,1,0:T(8,128)S(1)}, f32[1,16,128,128]{3,2,1,0:T(8,128)}, f32[16,128,128]{2,1,0:T(8,128)S(1)}) fusion(f32[16,128,128]{2,1,0:T(8,128)S(1)} %copy-done.12, f32[16,128,128]{2,1,0:T(8,128)S(1)} %get-tuple-element.44, f32[16,128,128]{2,1,0:T(8,128)S(1)} %get-tuple-element.43, f32[16,127,128]{2,1,0:T(8,128)S(1)} %bitcast.149, ...), kind=kLoop, calls=%fused_computation.26 | loop fusion | flops 5767168 | bytes 15728640 | tf_op jit(solution)/shard_map/add | solution.py:84
  42.5 1.0 copy-done.2
  43.4 1.2 slice_reduce_fusion.2
  44.8 0.9 fusion.44
  45.7 0.9 fusion.46
  46.6 0.9 fusion
  47.6 0.9 fusion.1
  48.6 3.4 %copy.200 = f32[2,4,4,16,256]{3,2,1,0,4:T(4,128)} copy(f32[2,4,4,16,256]{4,3,2,1,0:T(8,128)S(1)} %pad_maximum_fusion.2) | data formatting | bytes 1048576
  51.9 5.9 %reshape.43 = f32[256,512]{1,0:T(8,128)} reshape(f32[256,2,4,4,16]{4,3,2,1,0:T(4,128)} %bitcast.146) | data formatting | bytes 1048576
  57.9 24.4 %reduce-scatter.4.cloned.1.call-done = f32[64,512]{1,0:T(8,128)} async-done(((f32[256,512]{1,0:T(8,128)}), f32[64,512]{1,0:T(8,128)}) %reduce-scatter.4.cloned.1.call-update) | async-done | bytes 131088
  82.3 1.6 %reshape.44 = f32[64,2,4,4,16]{4,3,2,1,0:T(4,128)S(1)} reshape(f32[64,512]{1,0:T(8,128)} %reduce-scatter.4.cloned.1.call-done) | data formatting | bytes 262144
  84.0 0.8 reshape.49
  84.8 12.7 %all_to_all.24 = f32[8,1,4096]{2,1,0:T(1,128)S(1)} all-to-all(f32[8,1,4096]{2,1,0:T(1,128)S(1)} %reshape.49), channel_id=1, replica_groups=mesh['gx'=8,'gy'=4] {'gx'}, dimensions={0} | all-to-all | bytes 262144 | tf_op jit(solution)/shard_map/all_to_all | solution.py:113
  97.5 0.5 broadcast.137
  98.0 0.9 reduce.8
  98.9 0.7 reshape.50
  99.6 0.6 copy.204
  100.6 0.8 fusion.40
  101.7 0.8 fusion.38
  102.6 0.8 fusion.3
  103.4 0.8 fusion.2
  104.3 3.3 %copy.193 = f32[2,4,4,256,8]{4,2,1,0,3:T(4,128)} copy(f32[2,4,4,256,8]{3,4,2,1,0:T(8,128)S(1)} %pad_maximum_fusion.3) | data formatting | bytes 524288 | tf_op jit(solution)/shard_map/stack | solution.py:65
  107.6 7.3 %reshape.51 = f32[8,1,8192]{2,1,0:T(1,128)} reshape(f32[256,2,4,4,8]{4,3,2,1,0:T(4,128)} %bitcast.148) | data formatting | bytes 524288
  114.9 3.7 %all-to-all-start.1 = ((f32[8,1,8192]{2,1,0:T(1,128)}), f32[8,1,8192]{2,1,0:T(1,128)S(1)}, u32[]{:S(2)}, u32[]{:S(2)}) async-start(f32[8,1,8192]{2,1,0:T(1,128)} %reshape.51), calls=%async_computation.1 | async-start | bytes 524288 | tf_op jit(solution)/shard_map/all_to_all | solution.py:115
  118.6 1.9 %pad_maximum_fusion.1 = f32[3,16,128,128]{3,2,1,0:T(8,128)} fusion(f32[1,16,128,128]{3,2,1,0:T(8,128)S(1)} %copy-done.8, f32[1,16,128,128]{3,2,1,0:T(8,128)S(1)} %bitcast.151, f32[1,16,128,128]{3,2,1,0:T(8,128)S(1)} %bitcast.150), kind=kLoop, calls=%fused_computation.1 | loop fusion | flops 1572864 | bytes 6291456 | tf_op jit(solution)/shard_map/stack | solution.py:93
  120.5 6.0 %all-to-all-done.1 = f32[8,1,8192]{2,1,0:T(1,128)S(1)} async-done(((f32[8,1,8192]{2,1,0:T(1,128)}), f32[8,1,8192]{2,1,0:T(1,128)S(1)}, u32[]{:S(2)}, u32[]{:S(2)}) %all-to-all-start.1) | async-done | bytes 262176 | tf_op jit(solution)/shard_map/all_to_all | solution.py:115
  126.5 1.2 reduce.9
  127.7 6.9 %reshape.52 = f32[256,2,4,4,8]{4,3,2,1,0:T(4,128)} reshape(f32[8,8192]{1,0:T(8,128)S(1)} %reduce.9) | data formatting | bytes 524288
  134.6 5.2 %broadcast_multiply_fusion = f32[2,4,4,256,8]{4,2,1,0,3:T(4,128)} fusion(f32[256,2,4,4,8]{4,3,2,1,0:T(4,128)} %reshape.52), kind=kLoop, calls=%fused_computation.2 | loop fusion | flops 65536 | bytes 524288 | tf_op jit(solution)/shard_map/mul | solution.py:116
  139.8 3.6 %copy.194 = f32[2,4,4,8,32,8]{4,5,3,2,1,0:T(8,128)S(1)} copy(f32[2,4,4,8,32,8]{5,2,1,0,4,3:T(4,128)} %bitcast.147) | data formatting | bytes 524288 | tf_op jit(solution)/shard_map/mul | solution.py:116
  143.4 1.1 copy.195
  (61 shorter events, 1.6 us)
Async XLA Ops:
  7.2 75.1 %reduce-scatter.4.cloned.1.call-start = ((), (), s32[]{:S(2)}) async-start(), calls=%async_computation.3 | async-start | bytes 655360
  8.1 12.2 %collective-permute-start.1 = (f32[2,16,1,128]{3,1,2,0:T(8,128)S(1)}, f32[2,16,1,128]{3,1,2,0:T(8,128)S(1)}, u32[]{:S(2)}, u32[]{:S(2)}) collective-permute-start(f32[2,16,1,128]{3,1,2,0:T(8,128)S(1)} %bitcast.162), channel_id=1, source_target_pairs={{1,0},{2,1},{3,2},{5,4},{6,5},{7,6},{9,8},{10,9},{11,10},{13,12},{... | collective-permute-start | bytes 49160 | tf_op jit(solution)/shard_map/ppermute | solution.py:15
  10.4 9.9 %collective-permute-start = (f32[2,1,128,128]{3,2,1,0:T(8,128)S(1)}, f32[2,1,128,128]{3,2,1,0:T(8,128)S(1)}, u32[]{:S(2)}, u32[]{:S(2)}) collective-permute-start(f32[2,1,128,128]{3,2,1,0:T(8,128)S(1)} %slice.123), channel_id=1, source_target_pairs={{4,0},{8,4},{12,8},{16,12},{20,16},{24,20},{28,24},{5,1},{9,5},{13... | collective-permute-start | bytes 393224 | tf_op jit(solution)/shard_map/ppermute | solution.py:15
  11.7 5.8 %copy-start.18 = (f32[4]{0:T(128)S(1)}, f32[4]{0:T(128)}, u32[]{:S(2)}) copy-start(f32[4]{0:T(128)} %param.13) | copy-start | bytes 52
  14.0 6.3 %copy-start = (f32[3,16,128,128]{3,2,1,0:T(8,128)S(1)}, f32[3,16,128,128]{3,2,1,0:T(8,128)}, u32[]{:S(2)}) copy-start(f32[3,16,128,128]{3,2,1,0:T(8,128)} %param.7) | copy-start | bytes 9437188
  20.3 2.7 %copy-start.1 = (f32[16,128,128]{2,1,0:T(8,128)S(1)}, f32[16,128,128]{2,1,0:T(8,128)}, u32[]{:S(2)}) copy-start(f32[16,128,128]{2,1,0:T(8,128)} %slice_bitcast_fusion.2) | copy-start | bytes 3145732
  20.4 3.1 %copy-start.6 = (f32[3,16,128,128]{3,2,1,0:T(8,128)S(1)}, f32[3,16,128,128]{3,2,1,0:T(8,128)}, u32[]{:S(2)}) copy-start(f32[3,16,128,128]{3,2,1,0:T(8,128)} %param.8) | copy-start | bytes 9437188
  20.4 3.4 %copy-start.7 = (f32[16,127,128]{2,1,0:T(8,128)S(1)}, f32[16,127,128]{2,1,0:T(8,128)}, u32[]{:S(2)}) copy-start(f32[16,127,128]{2,1,0:T(8,128)} %get-tuple-element.54) | copy-start | bytes 3121156
  20.4 3.7 %copy-start.9 = (f32[15,128,128]{2,1,0:T(8,128)S(1)}, f32[15,128,128]{2,1,0:T(8,128)}, u32[]{:S(2)}) copy-start(f32[15,128,128]{2,1,0:T(8,128)} %get-tuple-element.46) | copy-start | bytes 2949124
  20.4 4.0 %copy-start.10 = (f32[15,128,128]{2,1,0:T(8,128)S(1)}, f32[15,128,128]{2,1,0:T(8,128)}, u32[]{:S(2)}) copy-start(f32[15,128,128]{2,1,0:T(8,128)} %get-tuple-element.48) | copy-start | bytes 2949124
  27.5 12.3 %copy-start.11 = (f32[3,16,128,128]{3,2,1,0:T(8,128)}, f32[3,16,128,128]{3,2,1,0:T(8,128)S(1)}, u32[]{:S(2)}) copy-start(f32[3,16,128,128]{3,2,1,0:T(8,128)S(1)} %pad_maximum_fusion) | copy-start | bytes 9437188
  27.5 12.2 %copy-start.12 = (f32[16,128,128]{2,1,0:T(8,128)S(1)}, f32[16,128,128]{2,1,0:T(8,128)}, u32[]{:S(2)}) copy-start(f32[16,128,128]{2,1,0:T(8,128)} %param.10) | copy-start | bytes 3145732
  27.5 12.2 %copy-start.13 = (f32[16,128,128]{2,1,0:T(8,128)S(1)}, f32[16,128,128]{2,1,0:T(8,128)}, u32[]{:S(2)}) copy-start(f32[16,128,128]{2,1,0:T(8,128)} %param.9) | copy-start | bytes 3145732
  27.6 9.2 %collective-permute-start.2 = (f32[2,16,1,128]{3,2,1,0:T(1,128)S(1)}, f32[2,16,1,128]{3,2,1,0:T(1,128)S(1)}, u32[]{:S(2)}, u32[]{:S(2)}) collective-permute-start(f32[2,16,1,128]{3,2,1,0:T(1,128)S(1)} %slice.139), channel_id=1, source_target_pairs={{0,1},{1,2},{2,3},{4,5},{5,6},{6,7},{8,9},{9,10},{10,11},{12,13},{... | collective-permute-start | bytes 49160 | tf_op jit(solution)/shard_map/ppermute | solution.py:15
  31.0 8.8 %collective-permute-start.3 = (f32[2,1,128,128]{3,2,1,0:T(8,128)S(1)}, f32[2,1,128,128]{3,2,1,0:T(8,128)S(1)}, u32[]{:S(2)}, u32[]{:S(2)}) collective-permute-start(f32[2,1,128,128]{3,2,1,0:T(8,128)S(1)} %pad_maximum_fusion.4), channel_id=1, source_target_pairs={{0,4},{4,8},{8,12},{12,16},{16,20},{20,24},{24,28},{1,5},{5,9},{9,... | collective-permute-start | bytes 393224 | tf_op jit(solution)/shard_map/ppermute | solution.py:15
  39.8 4.8 %copy-start.16 = (f32[4,4,16,128]{3,2,1,0:T(8,128)S(1)}, f32[4,4,16,128]{3,2,1,0:T(8,128)}, u32[]{:S(2)}) copy-start(f32[4,4,16,128]{3,2,1,0:T(8,128)} %param.12) | copy-start | bytes 393220
  39.8 4.8 %copy-start.17 = (f32[4,4,16,128]{3,2,1,0:T(8,128)S(1)}, f32[4,4,16,128]{3,2,1,0:T(8,128)}, u32[]{:S(2)}) copy-start(f32[4,4,16,128]{3,2,1,0:T(8,128)} %param.11) | copy-start | bytes 393220
  42.5 1.0 copy-start.2
  42.5 2.2 %copy-start.4 = (f32[16,128,128]{2,1,0:T(8,128)}, f32[16,128,128]{2,1,0:T(8,128)S(1)}, u32[]{:S(2)}) copy-start(f32[16,128,128]{2,1,0:T(8,128)S(1)} %get-tuple-element.42) | copy-start | bytes 3145732
  44.8 2.8 %copy-start.15 = (f32[4,4,16,128]{3,2,1,0:T(8,128)}, f32[4,4,16,128]{3,2,1,0:T(8,128)S(1)}, u32[]{:S(2)}) copy-start(f32[4,4,16,128]{3,2,1,0:T(8,128)S(1)} %get-tuple-element.62) | copy-start | bytes 393220
  44.8 7.2 %copy-start.14 = (f32[4,4,16,128]{3,2,1,0:T(8,128)}, f32[4,4,16,128]{3,2,1,0:T(8,128)S(1)}, u32[]{:S(2)}) copy-start(f32[4,4,16,128]{3,2,1,0:T(8,128)S(1)} %get-tuple-element.61) | copy-start | bytes 393220
  107.6 11.0 %copy-start.3 = (f32[16,128,128]{2,1,0:T(8,128)S(1)}, f32[16,128,128]{2,1,0:T(8,128)}, u32[]{:S(2)}) copy-start(f32[16,128,128]{2,1,0:T(8,128)} %copy-done.2) | copy-start | bytes 3145732
  107.6 11.0 %copy-start.5 = (f32[16,128,128]{2,1,0:T(8,128)S(1)}, f32[16,128,128]{2,1,0:T(8,128)}, u32[]{:S(2)}) copy-start(f32[16,128,128]{2,1,0:T(8,128)} %copy-done.4) | copy-start | bytes 3145732
  107.6 11.0 %copy-start.8 = (f32[1,16,128,128]{3,2,1,0:T(8,128)S(1)}, f32[1,16,128,128]{3,2,1,0:T(8,128)}, u32[]{:S(2)}) copy-start(f32[1,16,128,128]{3,2,1,0:T(8,128)} %get-tuple-element.41) | copy-start | bytes 3145732
  114.9 11.6 %all-to-all-start.1 = ((f32[8,1,8192]{2,1,0:T(1,128)}), f32[8,1,8192]{2,1,0:T(1,128)S(1)}, u32[]{:S(2)}, u32[]{:S(2)}) async-start(f32[8,1,8192]{2,1,0:T(1,128)} %reshape.51), calls=%async_computation.1 | async-start | bytes 524288 | tf_op jit(solution)/shard_map/all_to_all | solution.py:115
Sparse Core Ops, SparseCore 0:
  58.0 24.2 reduce-scatter.3
where the time goes:
time: 152 us; the launch traced here: 151 us
  local copies, waits for them, and re-layouts  52 us (34%)
  waiting for transfers between devices  33.3 us (22%)
  other arithmetic  16.4 us (11%)
  starting transfers between devices  15.3 us (10%)
  between operations  14.6 us (10%)
  blocking collectives  12.7 us (8%)
  matrix products  6.97 us (5%)
    unnamed x47, local copies, waits for them, and re-layouts  30.3 us
    unnamed x2, waiting for transfers between devices  24.4 us
    all_to_all x1, blocking collectives, per_device(): lax.all_to_all(reduced, 'gx', split_axis=4, concat_axis=3, tiled=True)  12.7 us
    ppermute x4, starting transfers between devices, passed_along(): return lax.ppermute(value, axis, pairs)  11.6 us
    slice x3, local copies, waits for them, and re-layouts, ahead_diff(): upper = lax.slice_in_dim(values, 1, values.shape[along], axis=along)  6.34 us
    all_to_all x1, waiting for transfers between devices, per_device(): lax.all_to_all(finished, 'gx', split_axis=3, concat_axis=4, tiled=True)  6 us
    mul x1, other arithmetic, per_device(): far_field = whole * scale  5.21 us
    all_to_all x1, starting transfers between devices, per_device(): lax.all_to_all(finished, 'gx', split_axis=3, concat_axis=4, tiled=True)  3.67 us
  transfers between devices with their start and end apart: 6, of which 3 were waited for; matrix products, arithmetic and copies ran while one was open for 8% of the time, Pallas kernels for 0%

commit v1 on v0

--- a/solution.py
+++ b/solution.py
@@ -110,7 +110,9 @@
     reduced = lax.psum_scatter(
         jnp.stack([part_real, part_imag]), "gy", scatter_dimension=4, tiled=True
     )
-    columns = lax.all_to_all(reduced, "gx", split_axis=4, concat_axis=3, tiled=True)
+    columns = jnp.concatenate(
+        lax.all_to_all(jnp.stack(jnp.split(reduced, lax.psum(1, "gx"), axis=4), 0), "gx", 0, 0), 3
+    )
     finished = second_section(columns[0], columns[1], cos_full, sin_full)
     whole = lax.all_to_all(finished, "gx", split_axis=3, concat_axis=4, tiled=True)
     far_field = whole * scale

time: 152 us -> 159 us (1.046)
  local copies, waits for them, and re-layouts: 52 us -> 58.3 us
    unnamed x47 -> x63, local copies, waits for them, and re-layouts: 30.3 us -> 38.5 us
    squeeze x1, local copies, waits for them, and re-layouts: 2.3 us -> 0.09 us  [per_device(): elec_x, elec_y, elec_z = (electric[0], electric[1], electric[2])]
  transfers between devices with their start and end apart: 6 -> 6, of which waited for: 3 -> 3; matrix products, arithmetic and copies ran while one was open for 8% -> 5% of each run, Pallas kernels for 0% -> 0%
where the time goes in v1:
time: 159 us
  local copies, waits for them, and re-layouts  58.3 us (37%)
  waiting for transfers between devices  33.9 us (21%)
  other arithmetic  16.7 us (11%)
  starting transfers between devices  15.3 us (10%)
  between operations  14.7 us (9%)
  blocking collectives  12.7 us (8%)
  matrix products  6.97 us (4%)
    unnamed x63, local copies, waits for them, and re-layouts  38.5 us
    unnamed x2, waiting for transfers between devices  24.9 us
    all_to_all x1, blocking collectives, per_device(): lax.all_to_all(jnp.stack(jnp.split(reduced, lax.psum(1, 'gx'), axis=4), 0...  12.7 us
    ppermute x4, starting transfers between devices, passed_along(): return lax.ppermute(value, axis, pairs)  11.6 us
    all_to_all x1, waiting for transfers between devices, per_device(): lax.all_to_all(finished, 'gx', split_axis=3, concat_axis=4, tiled=True)  6 us
    mul x1, other arithmetic, per_device(): far_field = whole * scale  5.2 us
    slice x3, local copies, waits for them, and re-layouts, ahead_diff(): upper = lax.slice_in_dim(values, 1, values.shape[along], axis=along)  4.97 us
    all_to_all x1, starting transfers between devices, per_device(): lax.all_to_all(finished, 'gx', split_axis=3, concat_axis=4, tiled=True)  3.67 us
  transfers between devices with their start and end apart: 6, of which 3 were waited for; matrix products, arithmetic and copies ran while one was open for 5% of the time, Pallas kernels for 0%

profile of v1, /device:TPU:0, one launch (start us, length us, event | category | flops | bytes accessed | tf_op | source)
XLA Modules:
  0.0 158.5 jit_solution(895731502851070218)
XLA Ops:
  7.2 1.1 slice.123
  8.3 1.3 collective-permute-start
  9.6 0.9 slice.127
  10.5 1.3 collective-permute-start.1
  11.8 3.3 %slice_bitcast_fusion.10 = (f32[15,128,128]{2,1,0:T(8,128)}, f32[1,15,128,128]{3,2,1,0:T(8,128)}, f32[15,128,128]{2,1,0:T(8,128)}) fusion(f32[3,16,128,128]{3,2,1,0:T(8,128)} %param.7), kind=kLoop, calls=%fused_computation.146 | loop fusion | bytes 4915200 | tf_op jit(solution)/shard_map/slice | solution.py:29
  15.3 1.0 copy-done.1
  16.2 1.6 fusion.97
  18.0 2.5 %slice_bitcast_fusion = (f32[16,128,128]{2,1,0:T(8,128)S(1)}, f32[1,16,128,128]{3,2,1,0:T(8,128)S(1)}, f32[16,128,128]{2,1,0:T(8,128)S(1)}) fusion(f32[3,16,128,128]{3,2,1,0:T(8,128)S(1)} %copy-done, f32[1,16,1,128]{3,2,1,0:T(1,128)S(1)} %bitcast.167, f32[1,16,127,128]{3,2,1,0:T(8,128)} %get-tuple-element.63, f32[1,1,128,128]{3,2,1,0:T(8,128)S(1)} %get-tuple-element.68, ...), kind=kLoop, calls=%fused_computation.55 | loop fusion | flops 1835008 | bytes 9437184 | tf_op jit(solution)/shard_map/squeeze | solution.py:69
  21.9 1.8 %fusion.22 = (f32[16,128,128]{2,1,0:T(8,128)S(1)}, f32[16,128,128]{2,1,0:T(8,128)S(1)}, f32[16,128,128]{2,1,0:T(8,128)S(1)}) fusion(f32[1,128,128]{2,1,0:T(8,128)S(1)} %get-tuple-element.66, f32[15,128,128]{2,1,0:T(8,128)S(1)} %copy-done.10, f32[16,1,128]{2,1,0:T(1,128)S(1)} %bitcast.168, f32[16,127,128]{2,1,0:T(8,128)S(1)} %copy-done.8, ...), kind=kLoop, calls=%fused_computation.38 | loop fusion | flops 4980736 | bytes 15728640 | tf_op jit(solution)/shard_map/sub | solution.py:78
  23.7 1.2 slice_reduce_fusion
  25.1 3.3 %collective-permute-start.2 = (f32[2,16,1,128]{3,2,1,0:T(1,128)S(1)}, f32[2,16,1,128]{3,2,1,0:T(1,128)S(1)}, u32[]{:S(2)}, u32[]{:S(2)}) collective-permute-start(f32[2,16,1,128]{3,2,1,0:T(1,128)S(1)} %slice.139), channel_id=1, source_target_pairs={{0,1},{1,2},{2,3},{4,5},{5,6},{6,7},{8,9},{9,10},{10,11},{12,13},{... | collective-permute-start | bytes 49160 | tf_op jit(solution)/shard_map/ppermute | solution.py:15
  28.5 5.7 %collective-permute-start.3 = (f32[2,1,128,128]{3,2,1,0:T(8,128)S(1)}, f32[2,1,128,128]{3,2,1,0:T(8,128)S(1)}, u32[]{:S(2)}, u32[]{:S(2)}) collective-permute-start(f32[2,1,128,128]{3,2,1,0:T(8,128)S(1)} %pad_maximum_fusion.4), channel_id=1, source_target_pairs={{0,4},{4,8},{8,12},{12,16},{16,20},{20,24},{24,28},{1,5},{5,9},{9,... | collective-permute-start | bytes 393224 | tf_op jit(solution)/shard_map/ppermute | solution.py:15
  34.4 2.9 %collective-permute-done.3 = f32[2,1,128,128]{3,2,1,0:T(8,128)S(1)} collective-permute-done((f32[2,1,128,128]{3,2,1,0:T(8,128)S(1)}, f32[2,1,128,128]{3,2,1,0:T(8,128)S(1)}, u32[]{:S(2)}, u32[]{:S(2)}) %collective-permute-start.3) | collective-permute-done | bytes 131104 | tf_op jit(solution)/shard_map/ppermute | solution.py:15
  37.4 2.6 %fusion.15 = (f32[16,128,128]{2,1,0:T(8,128)S(1)}, f32[1,16,128,128]{3,2,1,0:T(8,128)}, f32[16,128,128]{2,1,0:T(8,128)S(1)}) fusion(f32[16,128,128]{2,1,0:T(8,128)S(1)} %copy-done.13, f32[16,128,128]{2,1,0:T(8,128)S(1)} %get-tuple-element.44, f32[16,128,128]{2,1,0:T(8,128)S(1)} %get-tuple-element.43, f32[16,127,128]{2,1,0:T(8,128)S(1)} %bitcast.161, ...), kind=kLoop, calls=%fused_computation.26 | loop fusion | flops 5767168 | bytes 15728640 | tf_op jit(solution)/shard_map/add | solution.py:84
  40.0 1.0 copy-done.3
  41.0 1.2 slice_reduce_fusion.2
  42.3 0.9 fusion.44
  43.3 0.9 fusion.46
  44.2 0.9 fusion
  45.2 0.9 fusion.1
  46.1 3.4 %copy.192 = f32[2,4,4,16,256]{3,2,1,0,4:T(4,128)} copy(f32[2,4,4,16,256]{4,3,2,1,0:T(8,128)S(1)} %pad_maximum_fusion.2) | data formatting | bytes 1048576
  49.5 5.9 %reshape.48 = f32[256,512]{1,0:T(8,128)} reshape(f32[256,2,4,4,16]{4,3,2,1,0:T(4,128)} %bitcast.158) | data formatting | bytes 1048576
  55.5 24.9 %reduce-scatter.4.cloned.1.call-done = f32[64,512]{1,0:T(8,128)} async-done(((f32[256,512]{1,0:T(8,128)}), f32[64,512]{1,0:T(8,128)}) %reduce-scatter.4.cloned.1.call-update) | async-done | bytes 131088
  80.4 1.6 %reshape.49 = f32[64,2,4,4,16]{4,3,2,1,0:T(4,128)S(1)} reshape(f32[64,512]{1,0:T(8,128)} %reduce-scatter.4.cloned.1.call-done) | data formatting | bytes 262144
  82.0 0.8 fusion.96
  83.0 0.9 copy.196
  83.9 0.8 copy.197
  84.7 1.0 copy.198
  85.8 1.0 copy.199
  86.8 1.0 copy.200
  87.9 1.0 copy.201
  89.1 1.0 bitcast_dynamic-update-slice_fusion.6
  90.1 1.0 bitcast_dynamic-update-slice_fusion.5
  92.2 12.7 %all_to_all.14 = f32[8,1,4096]{2,1,0:T(1,128)S(1)} all-to-all(f32[8,1,4096]{2,1,0:T(1,128)S(1)} %reshape.54), channel_id=1, replica_groups=mesh['gx'=8,'gy'=4] {'gx'}, dimensions={0} | all-to-all | bytes 262144 | tf_op jit(solution)/shard_map/all_to_all | solution.py:114
  105.4 1.0 reduce.8
  108.8 0.8 fusion.40
  109.7 0.8 fusion.2
  110.5 0.8 fusion.3
  111.3 3.3 %copy.185 = f32[2,4,4,256,8]{4,2,1,0,3:T(4,128)} copy(f32[2,4,4,256,8]{3,4,2,1,0:T(8,128)S(1)} %pad_maximum_fusion.3) | data formatting | bytes 524288 | tf_op jit(solution)/shard_map/stack | solution.py:65
  114.7 7.3 %reshape.56 = f32[8,1,8192]{2,1,0:T(1,128)} reshape(f32[256,2,4,4,8]{4,3,2,1,0:T(4,128)} %bitcast.160) | data formatting | bytes 524288
  122.0 3.7 %all-to-all-start.1 = ((f32[8,1,8192]{2,1,0:T(1,128)}), f32[8,1,8192]{2,1,0:T(1,128)S(1)}, u32[]{:S(2)}, u32[]{:S(2)}) async-start(f32[8,1,8192]{2,1,0:T(1,128)} %reshape.56), calls=%async_computation.1 | async-start | bytes 524288 | tf_op jit(solution)/shard_map/all_to_all | solution.py:117
  125.7 1.9 %pad_maximum_fusion.1 = f32[3,16,128,128]{3,2,1,0:T(8,128)} fusion(f32[1,16,128,128]{3,2,1,0:T(8,128)S(1)} %copy-done.9, f32[1,16,128,128]{3,2,1,0:T(8,128)S(1)} %bitcast.163, f32[1,16,128,128]{3,2,1,0:T(8,128)S(1)} %bitcast.162), kind=kLoop, calls=%fused_computation.1 | loop fusion | flops 1572864 | bytes 6291456 | tf_op jit(solution)/shard_map/stack | solution.py:93
  127.6 6.0 %all-to-all-done.1 = f32[8,1,8192]{2,1,0:T(1,128)S(1)} async-done(((f32[8,1,8192]{2,1,0:T(1,128)}), f32[8,1,8192]{2,1,0:T(1,128)S(1)}, u32[]{:S(2)}, u32[]{:S(2)}) %all-to-all-start.1) | async-done | bytes 262176 | tf_op jit(solution)/shard_map/all_to_all | solution.py:117
  133.6 1.3 reduce.9
  134.9 6.9 %reshape.57 = f32[256,2,4,4,8]{4,3,2,1,0:T(4,128)} reshape(f32[8,8192]{1,0:T(8,128)S(1)} %reduce.9) | data formatting | bytes 524288
  141.8 5.2 %broadcast_multiply_fusion = f32[2,4,4,256,8]{4,2,1,0,3:T(4,128)} fusion(f32[256,2,4,4,8]{4,3,2,1,0:T(4,128)} %reshape.57), kind=kLoop, calls=%fused_computation.2 | loop fusion | flops 65536 | bytes 524288 | tf_op jit(solution)/shard_map/mul | solution.py:118
  147.0 3.6 %copy.186 = f32[2,4,4,8,32,8]{4,5,3,2,1,0:T(8,128)S(1)} copy(f32[2,4,4,8,32,8]{5,2,1,0,4,3:T(4,128)} %bitcast.159) | data formatting | bytes 524288 | tf_op jit(solution)/shard_map/mul | solution.py:118
  150.6 1.1 copy.187
  (80 shorter events, 6.6 us)
Async XLA Ops:
  7.2 8.0 %copy-start = (f32[3,16,128,128]{3,2,1,0:T(8,128)S(1)}, f32[3,16,128,128]{3,2,1,0:T(8,128)}, u32[]{:S(2)}) copy-start(f32[3,16,128,128]{3,2,1,0:T(8,128)} %param.7) | copy-start | bytes 9437188
  7.2 73.2 %reduce-scatter.4.cloned.1.call-start = ((), (), s32[]{:S(2)}) async-start(), calls=%async_computation.3 | async-start | bytes 655360
  8.3 9.6 %collective-permute-start = (f32[2,1,128,128]{3,2,1,0:T(8,128)S(1)}, f32[2,1,128,128]{3,2,1,0:T(8,128)S(1)}, u32[]{:S(2)}, u32[]{:S(2)}) collective-permute-start(f32[2,1,128,128]{3,2,1,0:T(8,128)S(1)} %slice.123), channel_id=1, source_target_pairs={{4,0},{8,4},{12,8},{16,12},{20,16},{24,20},{28,24},{5,1},{9,5},{13... | collective-permute-start | bytes 393224 | tf_op jit(solution)/shard_map/ppermute | solution.py:15
  10.5 7.3 %collective-permute-start.1 = (f32[2,16,1,128]{3,1,2,0:T(8,128)S(1)}, f32[2,16,1,128]{3,1,2,0:T(8,128)S(1)}, u32[]{:S(2)}, u32[]{:S(2)}) collective-permute-start(f32[2,16,1,128]{3,1,2,0:T(8,128)S(1)} %bitcast.174), channel_id=1, source_target_pairs={{1,0},{2,1},{3,2},{5,4},{6,5},{7,6},{9,8},{10,9},{11,10},{13,12},{... | collective-permute-start | bytes 49160 | tf_op jit(solution)/shard_map/ppermute | solution.py:15
  15.1 2.7 %copy-start.19 = (f32[4]{0:T(128)S(1)}, f32[4]{0:T(128)}, u32[]{:S(2)}) copy-start(f32[4]{0:T(128)} %param.13) | copy-start | bytes 52
  15.2 1.0 copy-start.1
  17.9 2.7 %copy-start.2 = (f32[16,128,128]{2,1,0:T(8,128)S(1)}, f32[16,128,128]{2,1,0:T(8,128)}, u32[]{:S(2)}) copy-start(f32[16,128,128]{2,1,0:T(8,128)} %copy-done.1) | copy-start | bytes 3145732
  17.9 3.1 %copy-start.7 = (f32[3,16,128,128]{3,2,1,0:T(8,128)S(1)}, f32[3,16,128,128]{3,2,1,0:T(8,128)}, u32[]{:S(2)}) copy-start(f32[3,16,128,128]{3,2,1,0:T(8,128)} %param.8) | copy-start | bytes 9437188
  17.9 3.4 %copy-start.8 = (f32[16,127,128]{2,1,0:T(8,128)S(1)}, f32[16,127,128]{2,1,0:T(8,128)}, u32[]{:S(2)}) copy-start(f32[16,127,128]{2,1,0:T(8,128)} %get-tuple-element.62) | copy-start | bytes 3121156
  17.9 3.7 %copy-start.10 = (f32[15,128,128]{2,1,0:T(8,128)S(1)}, f32[15,128,128]{2,1,0:T(8,128)}, u32[]{:S(2)}) copy-start(f32[15,128,128]{2,1,0:T(8,128)} %get-tuple-element.46) | copy-start | bytes 2949124
  18.0 4.0 %copy-start.11 = (f32[15,128,128]{2,1,0:T(8,128)S(1)}, f32[15,128,128]{2,1,0:T(8,128)}, u32[]{:S(2)}) copy-start(f32[15,128,128]{2,1,0:T(8,128)} %get-tuple-element.48) | copy-start | bytes 2949124
  25.1 12.3 %copy-start.12 = (f32[3,16,128,128]{3,2,1,0:T(8,128)}, f32[3,16,128,128]{3,2,1,0:T(8,128)S(1)}, u32[]{:S(2)}) copy-start(f32[3,16,128,128]{3,2,1,0:T(8,128)S(1)} %pad_maximum_fusion) | copy-start | bytes 9437188
  25.1 12.2 %copy-start.13 = (f32[16,128,128]{2,1,0:T(8,128)S(1)}, f32[16,128,128]{2,1,0:T(8,128)}, u32[]{:S(2)}) copy-start(f32[16,128,128]{2,1,0:T(8,128)} %param.10) | copy-start | bytes 3145732
  25.1 12.2 %copy-start.14 = (f32[16,128,128]{2,1,0:T(8,128)S(1)}, f32[16,128,128]{2,1,0:T(8,128)}, u32[]{:S(2)}) copy-start(f32[16,128,128]{2,1,0:T(8,128)} %param.9) | copy-start | bytes 3145732
  25.1 9.2 %collective-permute-start.2 = (f32[2,16,1,128]{3,2,1,0:T(1,128)S(1)}, f32[2,16,1,128]{3,2,1,0:T(1,128)S(1)}, u32[]{:S(2)}, u32[]{:S(2)}) collective-permute-start(f32[2,16,1,128]{3,2,1,0:T(1,128)S(1)} %slice.139), channel_id=1, source_target_pairs={{0,1},{1,2},{2,3},{4,5},{5,6},{6,7},{8,9},{9,10},{10,11},{12,13},{... | collective-permute-start | bytes 49160 | tf_op jit(solution)/shard_map/ppermute | solution.py:15
  28.5 8.8 %collective-permute-start.3 = (f32[2,1,128,128]{3,2,1,0:T(8,128)S(1)}, f32[2,1,128,128]{3,2,1,0:T(8,128)S(1)}, u32[]{:S(2)}, u32[]{:S(2)}) collective-permute-start(f32[2,1,128,128]{3,2,1,0:T(8,128)S(1)} %pad_maximum_fusion.4), channel_id=1, source_target_pairs={{0,4},{4,8},{8,12},{12,16},{16,20},{20,24},{24,28},{1,5},{5,9},{9,... | collective-permute-start | bytes 393224 | tf_op jit(solution)/shard_map/ppermute | solution.py:15
  37.4 4.8 %copy-start.17 = (f32[4,4,16,128]{3,2,1,0:T(8,128)S(1)}, f32[4,4,16,128]{3,2,1,0:T(8,128)}, u32[]{:S(2)}) copy-start(f32[4,4,16,128]{3,2,1,0:T(8,128)} %param.12) | copy-start | bytes 393220
  37.4 4.8 %copy-start.18 = (f32[4,4,16,128]{3,2,1,0:T(8,128)S(1)}, f32[4,4,16,128]{3,2,1,0:T(8,128)}, u32[]{:S(2)}) copy-start(f32[4,4,16,128]{3,2,1,0:T(8,128)} %param.11) | copy-start | bytes 393220
  40.0 1.0 copy-start.3
  40.0 2.2 %copy-start.5 = (f32[16,128,128]{2,1,0:T(8,128)}, f32[16,128,128]{2,1,0:T(8,128)S(1)}, u32[]{:S(2)}) copy-start(f32[16,128,128]{2,1,0:T(8,128)S(1)} %get-tuple-element.42) | copy-start | bytes 3145732
  42.3 2.8 %copy-start.15 = (f32[4,4,16,128]{3,2,1,0:T(8,128)}, f32[4,4,16,128]{3,2,1,0:T(8,128)S(1)}, u32[]{:S(2)}) copy-start(f32[4,4,16,128]{3,2,1,0:T(8,128)S(1)} %get-tuple-element.69) | copy-start | bytes 393220
  42.3 2.8 %copy-start.16 = (f32[4,4,16,128]{3,2,1,0:T(8,128)}, f32[4,4,16,128]{3,2,1,0:T(8,128)S(1)}, u32[]{:S(2)}) copy-start(f32[4,4,16,128]{3,2,1,0:T(8,128)S(1)} %get-tuple-element.70) | copy-start | bytes 393220
  114.7 11.0 %copy-start.4 = (f32[16,128,128]{2,1,0:T(8,128)S(1)}, f32[16,128,128]{2,1,0:T(8,128)}, u32[]{:S(2)}) copy-start(f32[16,128,128]{2,1,0:T(8,128)} %copy-done.3) | copy-start | bytes 3145732
  114.7 11.0 %copy-start.6 = (f32[16,128,128]{2,1,0:T(8,128)S(1)}, f32[16,128,128]{2,1,0:T(8,128)}, u32[]{:S(2)}) copy-start(f32[16,128,128]{2,1,0:T(8,128)} %copy-done.5) | copy-start | bytes 3145732
  114.7 11.0 %copy-start.9 = (f32[1,16,128,128]{3,2,1,0:T(8,128)S(1)}, f32[1,16,128,128]{3,2,1,0:T(8,128)}, u32[]{:S(2)}) copy-start(f32[1,16,128,128]{3,2,1,0:T(8,128)} %get-tuple-element.41) | copy-start | bytes 3145732
  122.0 11.6 %all-to-all-start.1 = ((f32[8,1,8192]{2,1,0:T(1,128)}), f32[8,1,8192]{2,1,0:T(1,128)S(1)}, u32[]{:S(2)}, u32[]{:S(2)}) async-start(f32[8,1,8192]{2,1,0:T(1,128)} %reshape.56), calls=%async_computation.1 | async-start | bytes 524288 | tf_op jit(solution)/shard_map/all_to_all | solution.py:117
Sparse Core Ops, SparseCore 0:
  55.6 24.7 reduce-scatter.3
